TPU v7x, 512 devices: a whole 4x4x16 slice. The times are simulated.
512 devices in a mesh: dp: 4 (over y), row: 16 (over x, z_lo), col: 8 (over z_hi, core).
Axes of the slice: x: 4, y: 4, z: 16 (z_hi: 4, z_lo: 4; z = z_hi * 4 + z_lo), core: 2. Of those that a mesh axis runs over, the one named last changes fastest.
Arguments:
- grad_parts: float32 [4, 4, 1024, 10240], P('dp', None, 'row', 'col'), may hold values from -120 to 120, as said below
- gauss_noise: float32 [4096, 10240], P(('dp', 'row'), 'col'), may hold values from -6 to 6
- blt_buffers: float32 [4, 4096, 10240], P(None, ('dp', 'row'), 'col'), may hold values from -4 to 4
- blt_decays: float32 [4], replicated, may hold values from 0.2 to 0.98
- blt_weights: float32 [4], replicated, may hold values from 0.1 to 0.6
- master_weights: float32 [4096, 10240], P(('dp', 'row'), 'col'), may hold values from -4 to 4
- row_stat: float32 [4096], P(('dp', 'row')), may hold values from 0.05 to 0.5
- col_stat: float32 [10240], P('col'), may hold values from 0.05 to 0.5
Outputs:
- direction: float32 [4096, 10240], P(('dp', 'row'), 'col')
- weight_copy: bfloat16 [4096, 10240], P(('dp', 'row'), 'col')
- new_buffers: float32 [4, 4096, 10240], P(None, ('dp', 'row'), 'col')
- new_row_stat: float32 [4096], P(('dp', 'row'))
- new_col_stat: float32 [10240], P('col')
Inputs may be any that keep to these rules, and one draw needn't show every extreme that they name: `grad_parts`: finite real values.
All inputs are finite; a program needn't handle non-finite values.
Results may differ from a plain program's by a relative error of at most 0.001.
Values sent between devices are 32-bit elements; how exact they have to be, the bound alone decides.
No kernel may reach another device: no remote copies, remote signals or barrier semaphores. Data moves between devices by JAX's collectives and lax.ppermute only.
A program may use at most 64 MiB of HBM per device.

v0:
```python
import functools

import jax
import jax.numpy as jnp
from jax import lax
from jax.sharding import Mesh
from jax.sharding import PartitionSpec as P

D = 4096
FF = 10240
COL = ("col_0", "col_1")


NOISE_STD = 2.0
DECAY_RATE = 0.85
LEARN_RATE = 0.01
TINY_TERM = 1e-30


def in_blocks(shard, dim, length):
    dims = shard.shape
    pieces = shard.reshape(*dims[:dim], length, dims[dim] // length, *dims[dim + 1 :])
    return jnp.moveaxis(pieces, dim, 0)


def sent_and_summed(shard, axis, dim):
    pieces = in_blocks(shard, dim, lax.axis_size(axis))
    arrived = lax.all_to_all(pieces, axis, split_axis=0, concat_axis=0, tiled=True)
    return arrived.sum(axis=0)


def one_axis_at_a_time(shard, axes):
    return functools.reduce(lax.psum, axes, shard)


def copy_for_each(shard, axis):
    copies = jnp.broadcast_to(shard, (lax.axis_size(axis), *shard.shape))
    return lax.all_to_all(copies, axis, split_axis=0, concat_axis=0, tiled=True)


def of_everyone(shard, axis):
    everything = copy_for_each(shard, axis)
    return jnp.sum(everything, axis=0)


def per_device(
    grad_parts,
    gauss_noise,
    blt_buffers,
    blt_decays,
    blt_weights,
    master_weights,
    row_stat,
    col_stat,
):
    local_rows = grad_parts.shape[2]
    local_cols = grad_parts.shape[3]
    grad_sum = sent_and_summed(grad_parts, "dp", 1).reshape(local_rows, local_cols)
    correlated = gauss_noise - jnp.sum(blt_buffers * blt_weights[:, None, None], axis=0)
    new_buffers = blt_decays[:, None, None] * blt_buffers + correlated[None]
    noisy = grad_sum + NOISE_STD * correlated
    squares = noisy * noisy
    row_totals = one_axis_at_a_time(jnp.sum(squares, axis=1), COL)
    col_totals = of_everyone(jnp.sum(squares, axis=0), ("dp", "row"))
    new_row = DECAY_RATE * row_stat + (1.0 - DECAY_RATE) * (row_totals / FF + TINY_TERM)
    new_col = DECAY_RATE * col_stat + (1.0 - DECAY_RATE) * (col_totals / D + TINY_TERM)
    row_mean = of_everyone(jnp.sum(new_row), ("dp", "row")) / D
    direction = noisy / jnp.sqrt(new_row[:, None] * new_col[None, :] / row_mean)
    weight_copy = (master_weights - LEARN_RATE * direction).astype(jnp.bfloat16)
    return (direction, weight_copy, new_buffers, new_row, new_col)


def solution(mesh):
    finer = Mesh(
        mesh.devices.reshape(mesh.shape["dp"], mesh.shape["row"], 4, 2),
        ("dp", "row", "col_0", "col_1"),
    )
    return jax.shard_map(
        per_device,
        mesh=finer,
        in_specs=(
            P("dp", None, "row", COL),
            P(("dp", "row"), COL),
            P(None, ("dp", "row"), COL),
            P(),
            P(),
            P(("dp", "row"), COL),
            P(("dp", "row")),
            P(COL),
        ),
        out_specs=(
            P(("dp", "row"), COL),
            P(("dp", "row"), COL),
            P(None, ("dp", "row"), COL),
            P(("dp", "row")),
            P(COL),
        ),
        check_vma=False,
    )
```

profile of v0, /device:TPU:2, one launch (start us, length us, event | category | flops | bytes accessed | tf_op | source)
XLA Modules:
  0.0 85.7 jit_solution(17448287411627924288)
XLA Ops:
  0.6 0.0 copy-start
  0.6 0.0 copy-start.5
  0.7 4.6 %all-to-all-start = ((f32[4,1,1,64,1280]{4,3,2,1,0:T(8,128)}), f32[4,1,1,64,1280]{4,3,2,1,0:T(8,128)S(1)}, u32[]{:S(2)}, u32[]{:S(2)}) async-start(f32[4,1,1,64,1280]{4,3,2,1,0:T(8,128)} %bitcast.1), calls=%async_computation | async-start | bytes 2621440 | tf_op jit(solution)/shard_map/all_to_all | solution.py:28
  5.3 0.0 copy-done
  5.3 0.0 copy-done.5
  5.3 0.9 %multiply_reduce_fusion = f32[64,1280]{1,0:T(8,128)} fusion(f32[4,64,1280]{2,1,0:T(8,128)S(1)} %copy-done, f32[4]{0:T(128)S(1)} %copy-done.5), kind=kLoop, calls=%fused_computation.1 | loop fusion | flops 573440 | bytes 1638416 | tf_op jit(solution)/shard_map/reduce_sum | solution.py:59
  6.1 0.0 copy-start.7
  6.1 17.0 %all-to-all-done = f32[4,1,1,64,1280]{4,3,2,1,0:T(8,128)S(1)} async-done(((f32[4,1,1,64,1280]{4,3,2,1,0:T(8,128)}), f32[4,1,1,64,1280]{4,3,2,1,0:T(8,128)S(1)}, u32[]{:S(2)}, u32[]{:S(2)}) %all-to-all-start) | async-done | bytes 1310752 | tf_op jit(solution)/shard_map/all_to_all | solution.py:28
  23.2 0.1 reduce_sum.63
  23.3 0.0 copy-start.6
  23.3 1.3 %multiply_reduce_fusion.1 = (f32[1280]{0:T(1024)S(1)}, f32[64]{0:T(128)S(1)}, f32[64,1280]{1,0:T(8,128)S(1)}) fusion(f32[64,1280]{1,0:T(8,128)S(1)} %reduce_sum.63, f32[64,1280]{1,0:T(8,128)} %param.9, f32[64,1280]{1,0:T(8,128)} %multiply_reduce_fusion), kind=kLoop, calls=%fused_computation.5 | loop fusion | flops 490176 | bytes 1316096 | tf_op jit(solution)/shard_map/reduce_sum | solution.py:64
  24.5 21.3 %psum.14 = f32[64]{0:T(128)S(1)} all-reduce(f32[64]{0:T(128)S(1)} %get-tuple-element.6), channel_id=1, replica_groups=mesh['dp'=4,'row'=16,'col_0'=4,'col_1'=2] {'col_0'}, use_global_device_ids=true, to_apply=%region_3.0 | all-reduce | flops 64 | bytes 512 | tf_op jit(solution)/shard_map/psum | solution.py:33
  45.8 2.5 %psum.15 = f32[64]{0:T(128)S(1)} all-reduce(f32[64]{0:T(128)S(1)} %psum.14), channel_id=1, replica_groups=mesh['dp'=4,'row'=16,'col_0'=4,'col_1'=2] {'col_1'}, use_global_device_ids=true, to_apply=%region_4.0 | all-reduce | flops 64 | bytes 512 | tf_op jit(solution)/shard_map/psum | solution.py:33
  48.2 0.0 copy-done.7
  48.2 0.6 fusion
  48.8 0.7 broadcast_in_dim.5
  49.5 16.0 %all_to_all.17 = f32[64,1,1]{2,1,0:T(1,128)S(1)} all-to-all(f32[64,1,1]{2,1,0:T(1,128)S(1)} %broadcast_in_dim.5), channel_id=1, replica_groups=mesh['dp'=4,'row'=16,'col_0'=4,'col_1'=2] {'dp','row'}, dimensions={0} | all-to-all | bytes 512 | tf_op jit(solution)/shard_map/all_to_all | solution.py:38
  65.5 0.9 %broadcast_in_dim.4 = f32[64,1,1280]{2,1,0:T(1,128)} broadcast(f32[1280]{0:T(1024)S(1)} %get-tuple-element.5), dimensions={2} | broadcast | bytes 332800 | tf_op jit(solution)/shard_map/broadcast_in_dim | solution.py:37
  66.4 5.5 %all-to-all-start.1 = ((f32[64,1,1280]{2,1,0:T(1,128)}), f32[64,1,1280]{2,1,0:T(1,128)S(1)}, u32[]{:S(2)}, u32[]{:S(2)}) async-start(f32[64,1,1280]{2,1,0:T(1,128)} %broadcast_in_dim.4), calls=%async_computation.1 | async-start | bytes 655360 | tf_op jit(solution)/shard_map/all_to_all | solution.py:38
  72.0 0.0 copy-done.6
  72.0 0.0 copy-start.3
  72.0 0.0 copy-start.1
  72.0 1.2 %multiply_add_fusion = f32[4,64,1280]{2,1,0:T(8,128)} fusion(f32[4,64,1280]{2,1,0:T(8,128)S(1)} %copy-done, f32[64,1280]{1,0:T(8,128)S(1)} %get-tuple-element.11, f32[4]{0:T(128)S(1)} %copy-done.6), kind=kLoop, calls=%fused_computation | loop fusion | flops 655360 | bytes 2949136 | tf_op jit(solution)/shard_map/add | solution.py:60
  73.2 0.7 reduce_sum.69
  74.5 9.9 %all-to-all-done.1 = f32[64,1,1280]{2,1,0:T(1,128)S(1)} async-done(((f32[64,1,1280]{2,1,0:T(1,128)}), f32[64,1,1280]{2,1,0:T(1,128)S(1)}, u32[]{:S(2)}, u32[]{:S(2)}) %all-to-all-start.1) | async-done | bytes 327712 | tf_op jit(solution)/shard_map/all_to_all | solution.py:38
  84.4 0.2 reduce_sum.67
  84.7 0.0 copy-done.3
  84.7 0.0 copy-start.2
  84.7 0.0 copy-done.4
  84.7 0.0 copy-done.1
  84.7 1.0 %subtract_convert_fusion = (bf16[64,1280]{1,0:T(8,128)(2,1)}, f32[64,1280]{1,0:T(8,128)}) fusion(f32[64,1280]{1,0:T(8,128)S(1)} %copy-done.1, f32[]{:T(128)S(6)} %div.28, f32[1280]{0:T(1024)S(1)} %multiply_add_fusion.2, f32[64]{0:T(128)S(1)} %get-tuple-element.10, f32[64,1280]{1,0:T(8,128)S(1)} %reduce_sum.63, f32[64,1280]{1,0:T(8,128)S(1)} %get-tuple-element.11), kind=kLoop, calls=%fused_computation.2 | loop fusion | flops 655360 | bytes 1479940 | tf_op jit(solution)/shard_map/convert_element_type | solution.py:69
  85.7 0.0 copy-done.2
  (2 shorter events, 0.0 us)
Async XLA Ops:
  0.6 4.6 %copy-start = (f32[4,64,1280]{2,1,0:T(8,128)S(1)}, f32[4,64,1280]{2,1,0:T(8,128)}, u32[]{:S(2)}) copy-start(f32[4,64,1280]{2,1,0:T(8,128)} %param.10) | copy-start | bytes 3932164
  0.6 4.6 %copy-start.5 = (f32[4]{0:T(128)S(1)}, f32[4]{0:T(128)}, u32[]{:S(2)}) copy-start(f32[4]{0:T(128)} %param.12) | copy-start | bytes 52
  0.7 22.5 %all-to-all-start = ((f32[4,1,1,64,1280]{4,3,2,1,0:T(8,128)}), f32[4,1,1,64,1280]{4,3,2,1,0:T(8,128)S(1)}, u32[]{:S(2)}, u32[]{:S(2)}) async-start(f32[4,1,1,64,1280]{4,3,2,1,0:T(8,128)} %bitcast.1), calls=%async_computation | async-start | bytes 2621440 | tf_op jit(solution)/shard_map/all_to_all | solution.py:28
  6.1 42.1 %copy-start.7 = (f32[64]{0:T(128)S(1)}, f32[64]{0:T(128)}, u32[]{:S(2)}) copy-start(f32[64]{0:T(128)} %param.14) | copy-start | bytes 772
  23.3 48.7 %copy-start.6 = (f32[4]{0:T(128)S(1)}, f32[4]{0:T(128)}, u32[]{:S(2)}) copy-start(f32[4]{0:T(128)} %param.11) | copy-start | bytes 52
  48.8 35.9 %copy-start.4 = (f32[64]{0:T(128)}, f32[64]{0:T(128)S(1)}, u32[]{:S(2)}) copy-start(f32[64]{0:T(128)S(1)} %get-tuple-element.10) | copy-start | bytes 772
  66.4 18.0 %all-to-all-start.1 = ((f32[64,1,1280]{2,1,0:T(1,128)}), f32[64,1,1280]{2,1,0:T(1,128)S(1)}, u32[]{:S(2)}, u32[]{:S(2)}) async-start(f32[64,1,1280]{2,1,0:T(1,128)} %broadcast_in_dim.4), calls=%async_computation.1 | async-start | bytes 655360 | tf_op jit(solution)/shard_map/all_to_all | solution.py:38
  72.0 12.7 %copy-start.3 = (f32[1280]{0:T(1024)S(1)}, f32[1280]{0:T(1024)}, u32[]{:S(2)}) copy-start(f32[1280]{0:T(1024)} %param.15) | copy-start | bytes 15364
  72.0 12.7 %copy-start.1 = (f32[64,1280]{1,0:T(8,128)S(1)}, f32[64,1280]{1,0:T(8,128)}, u32[]{:S(2)}) copy-start(f32[64,1280]{1,0:T(8,128)} %param.13) | copy-start | bytes 983044
  84.7 1.0 %copy-start.2 = (f32[1280]{0:T(1024)}, f32[1280]{0:T(1024)S(1)}, u32[]{:S(2)}) copy-start(f32[1280]{0:T(1024)S(1)} %multiply_add_fusion.2) | copy-start | bytes 15364
where the time goes:
time: 86 us; the launch traced here: 85.7 us
  blocking collectives  39.7 us (46%)
  waiting for transfers between devices  26.9 us (31%)
  starting transfers between devices  10.1 us (12%)
  other arithmetic  5.9 us (7%)
  local copies, waits for them, and re-layouts  1.6 us (2%)
  between operations  1.39 us (2%)
    psum x2, blocking collectives, one_axis_at_a_time(): return functools.reduce(lax.psum, axes, shard)  23.7 us
    all_to_all x1, waiting for transfers between devices, sent_and_summed(): lax.all_to_all(pieces, axis, split_axis=0, concat_axis=0, tiled=True)  17 us
    all_to_all x1, blocking collectives, copy_for_each(): return lax.all_to_all(copies, axis, split_axis=0, concat_axis=0, tiled=True)  16 us
    all_to_all x1, waiting for transfers between devices, copy_for_each(): return lax.all_to_all(copies, axis, split_axis=0, concat_axis=0, tiled=True)  9.91 us
    all_to_all x1, starting transfers between devices, copy_for_each(): return lax.all_to_all(copies, axis, split_axis=0, concat_axis=0, tiled=True)  5.51 us
    all_to_all x1, starting transfers between devices, sent_and_summed(): lax.all_to_all(pieces, axis, split_axis=0, concat_axis=0, tiled=True)  4.61 us
  transfers between devices with their start and end apart: 2, of which 2 were waited for; matrix products, arithmetic and copies ran while one was open for 3% of the time, Pallas kernels for 0%

commit v1 on v0

v1 whole, which is shorter than its diff:
```python
import jax
import jax.numpy as jnp
from jax import lax
from jax.sharding import Mesh
from jax.sharding import PartitionSpec as P


D = 4096
FF = 10240
NOISE_STD = 2.0
DECAY_RATE = 0.85
LEARN_RATE = 0.01
TINY_TERM = 1e-30

ROW = ("x", "zl")
COL = ("zh", "core")
DEPTH = ("zl", "zh", "core")
PLANE = ("dp", "x")


def from_all(shard, axes):
    n = lax.axis_size(axes)
    copies = jnp.broadcast_to(shard[None], (n, *shard.shape))
    return lax.all_to_all(copies, axes, split_axis=0, concat_axis=0, tiled=True)


def per_device(
    grad_parts,
    gauss_noise,
    blt_buffers,
    blt_decays,
    blt_weights,
    master_weights,
    row_stat,
    col_stat,
):
    rows, cols = gauss_noise.shape
    n_col = lax.axis_size(COL)
    arrived = lax.all_to_all(
        grad_parts.reshape(-1, rows, cols), "dp", split_axis=0, concat_axis=0, tiled=True
    )
    correlated = gauss_noise - jnp.sum(blt_buffers * blt_weights[:, None, None], axis=0)
    new_buffers = blt_decays[:, None, None] * blt_buffers + correlated[None]
    arrived, correlated, new_buffers = lax.optimization_barrier((arrived, correlated, new_buffers))
    noisy = arrived.sum(axis=0) + NOISE_STD * correlated
    squares = noisy * noisy
    share = DECAY_RATE / n_col * row_stat + (1.0 - DECAY_RATE) * (
        jnp.sum(squares, axis=1) / FF + TINY_TERM / n_col
    )
    col_part = jnp.sum(squares, axis=0)
    shares = from_all(share, DEPTH)
    col_parts = from_all(col_part, "zl")
    shares = shares.reshape(-1, n_col, rows).sum(axis=1)
    new_row = lax.dynamic_index_in_dim(shares, lax.axis_index("zl"), 0, keepdims=False)
    packed = jnp.concatenate([col_parts.sum(axis=0), shares.sum(axis=0)])
    packs = from_all(packed, PLANE).sum(axis=0)
    new_col = DECAY_RATE * col_stat + (1.0 - DECAY_RATE) * (packs[:cols] / D + TINY_TERM)
    row_mean = jnp.sum(packs[cols:]) / D
    direction = noisy / jnp.sqrt(new_row[:, None] * new_col[None, :] / row_mean)
    weight_copy = (master_weights - LEARN_RATE * direction).astype(jnp.bfloat16)
    return (direction, weight_copy, new_buffers, new_row, new_col)


def solution(mesh):
    finer = Mesh(
        mesh.devices.reshape(mesh.shape["dp"], 4, 4, 4, 2),
        ("dp", "x", "zl", "zh", "core"),
    )
    rows = ("dp", *ROW)
    return jax.shard_map(
        per_device,
        mesh=finer,
        in_specs=(
            P("dp", None, ROW, COL),
            P(rows, COL),
            P(None, rows, COL),
            P(),
            P(),
            P(rows, COL),
            P(rows),
            P(COL),
        ),
        out_specs=(P(rows, COL), P(rows, COL), P(None, rows, COL), P(rows), P(COL)),
        check_vma=False,
    )
```

time: 86 us -> 76.5 us (0.89)
  blocking collectives: 39.7 us -> 0 us
  starting transfers between devices: 10.1 us -> 28.8 us
  waiting for transfers between devices: 26.9 us -> 39.8 us
  other arithmetic: 5.9 us -> 3.34 us
  local copies, waits for them, and re-layouts: 1.6 us -> 2.76 us
    psum x2 -> x0, blocking collectives: 23.7 us -> none  [one_axis_at_a_time(): return functools.reduce(lax.psum, axes, shard)]
    all_to_all x2 -> x4, starting transfers between devices: 10.1 us -> 28.8 us  [the longest x3 24.2 us: from_all(): return lax.all_to_all(copies, axes, split_axis=0, concat_axis=0, tiled=True)]
    all_to_all x1 -> x0, blocking collectives: 16 us -> none  [copy_for_each(): return lax.all_to_all(copies, axis, split_axis=0, concat_axis=0, tiled=True)]
    all_to_all x2 -> x4, waiting for transfers between devices: 26.9 us -> 39.8 us  [the longest x3 24.1 us: from_all(): return lax.all_to_all(copies, axes, split_axis=0, concat_axis=0, tiled=True)]
    reduce_sum x5 -> x7, other arithmetic: 2.83 us -> 0.98 us  [the longest x1 0.6 us: per_device(): row_mean = jnp.sum(packs[cols:]) / D]
    broadcast_in_dim x2 -> x3, local copies, waits for them, and re-layouts: 1.56 us -> 1.92 us  [from_all(): copies = jnp.broadcast_to(shard[None], (n, *shard.shape))]
  transfers between devices with their start and end apart: 2 -> 4, of which waited for: 2 -> 4; matrix products, arithmetic and copies ran while one was open for 3% -> 2% of each run, Pallas kernels for 0% -> 0%
where the time goes in v1:
time: 76.5 us; the launch traced here: 76.1 us
  waiting for transfers between devices  39.8 us (52%)
  starting transfers between devices  28.8 us (38%)
  other arithmetic  3.34 us (4%)
  local copies, waits for them, and re-layouts  2.76 us (4%)
  between operations  1.41 us (2%)
    all_to_all x3, starting transfers between devices, from_all(): return lax.all_to_all(copies, axes, split_axis=0, concat_axis=0, tiled=True)  24.2 us
    all_to_all x3, waiting for transfers between devices, from_all(): return lax.all_to_all(copies, axes, split_axis=0, concat_axis=0, tiled=True)  24.1 us
    all_to_all x1, waiting for transfers between devices, per_device(): lax.all_to_all(grad_parts.reshape(-1, rows, cols), 'dp', split_axis=0, co...  15.6 us
    all_to_all x1, starting transfers between devices, per_device(): lax.all_to_all(grad_parts.reshape(-1, rows, cols), 'dp', split_axis=0, co...  4.61 us
    broadcast_in_dim x3, local copies, waits for them, and re-layouts, from_all(): copies = jnp.broadcast_to(shard[None], (n, *shard.shape))  1.92 us
  transfers between devices with their start and end apart: 4, of which 4 were waited for; matrix products, arithmetic and copies ran while one was open for 2% of the time, Pallas kernels for 0%

profile of v1, /device:TPU:2, one launch (start us, length us, event | category | flops | bytes accessed | tf_op | source)
XLA Modules:
  0.0 76.1 jit_solution(6103850258926145940)
XLA Ops:
  0.6 0.0 copy-start
  0.6 0.0 copy-start.6
  0.7 4.6 %all-to-all-start = ((f32[4,64,1280]{2,1,0:T(8,128)}), f32[4,64,1280]{2,1,0:T(8,128)S(1)}, u32[]{:S(2)}, u32[]{:S(2)}) async-start(f32[4,64,1280]{2,1,0:T(8,128)} %bitcast.7), calls=%async_computation | async-start | bytes 2621440 | tf_op jit(solution)/shard_map/all_to_all | solution.py:39
  5.3 0.0 copy-done
  5.3 0.0 copy-done.6
  5.3 0.0 copy-start.2
  5.3 0.0 copy-start.7
  5.3 0.2 multiply_reduce_fusion
  5.4 0.8 %copy-done.2 = f32[64,1280]{1,0:T(8,128)S(1)} copy-done((f32[64,1280]{1,0:T(8,128)S(1)}, f32[64,1280]{1,0:T(8,128)}, u32[]{:S(2)}) %copy-start.2) | copy-done | bytes 327704
  6.3 0.0 copy-done.7
  6.3 1.2 %multiply_add_fusion = f32[4,64,1280]{2,1,0:T(8,128)} fusion(f32[4,64,1280]{2,1,0:T(8,128)S(1)} %copy-done, f32[64,1280]{1,0:T(8,128)S(1)} %sub.6, f32[4]{0:T(128)S(1)} %copy-done.7), kind=kLoop, calls=%fused_computation | loop fusion | flops 655360 | bytes 2949136 | tf_op jit(solution)/shard_map/add | solution.py:43
  7.5 15.6 %all-to-all-done = f32[4,64,1280]{2,1,0:T(8,128)S(1)} async-done(((f32[4,64,1280]{2,1,0:T(8,128)}), f32[4,64,1280]{2,1,0:T(8,128)S(1)}, u32[]{:S(2)}, u32[]{:S(2)}) %all-to-all-start) | async-done | bytes 1310752 | tf_op jit(solution)/shard_map/all_to_all | solution.py:39
  23.2 0.1 reduce_sum.82
  23.3 0.2 multiply_reduce_fusion.1
  23.4 0.0 copy-done.8
  23.4 0.6 broadcast_in_dim.6
  24.0 15.5 %all-to-all-start.1 = ((f32[32,1,64]{2,1,0:T(1,128)}), f32[32,1,64]{2,1,0:T(1,128)S(1)}, u32[]{:S(2)}, u32[]{:S(2)}) async-start(f32[32,1,64]{2,1,0:T(1,128)} %broadcast_in_dim.6), calls=%async_computation.1 | async-start | bytes 32768 | tf_op jit(solution)/shard_map/all_to_all | solution.py:24
  39.5 12.2 %all-to-all-done.1 = f32[32,1,64]{2,1,0:T(1,128)S(1)} async-done(((f32[32,1,64]{2,1,0:T(1,128)}), f32[32,1,64]{2,1,0:T(1,128)S(1)}, u32[]{:S(2)}, u32[]{:S(2)}) %all-to-all-start.1) | async-done | bytes 8224 | tf_op jit(solution)/shard_map/all_to_all | solution.py:24
  51.8 0.6 broadcast_in_dim.7
  52.4 3.3 %all-to-all-start.2 = ((f32[4,1,1280]{2,1,0:T(1,128)}), f32[4,1,1280]{2,1,0:T(1,128)S(1)}, u32[]{:S(2)}, u32[]{:S(2)}) async-start(f32[4,1,1280]{2,1,0:T(1,128)} %broadcast_in_dim.7), calls=%async_computation.2 | async-start | bytes 40960 | tf_op jit(solution)/shard_map/all_to_all | solution.py:24
  55.7 5.5 %all-to-all-done.2 = f32[4,1,1280]{2,1,0:T(1,128)S(1)} async-done(((f32[4,1,1280]{2,1,0:T(1,128)}), f32[4,1,1280]{2,1,0:T(1,128)S(1)}, u32[]{:S(2)}, u32[]{:S(2)}) %all-to-all-start.2) | async-done | bytes 20512 | tf_op jit(solution)/shard_map/all_to_all | solution.py:24
  61.3 0.7 broadcast_in_dim.8
  62.0 5.5 %all-to-all-start.3 = ((f32[16,1,1344]{2,1,0:T(1,128)}), f32[16,1,1344]{2,1,0:T(1,128)S(1)}, u32[]{:S(2)}, u32[]{:S(2)}) async-start(f32[16,1,1344]{2,1,0:T(1,128)} %broadcast_in_dim.8), calls=%async_computation.3 | async-start | bytes 180224 | tf_op jit(solution)/shard_map/all_to_all | solution.py:24
  67.4 0.0 copy-start.5
  67.4 6.4 %all-to-all-done.3 = f32[16,1,1344]{2,1,0:T(1,128)S(1)} async-done(((f32[16,1,1344]{2,1,0:T(1,128)}), f32[16,1,1344]{2,1,0:T(1,128)S(1)}, u32[]{:S(2)}, u32[]{:S(2)}) %all-to-all-start.3) | async-done | bytes 86048 | tf_op jit(solution)/shard_map/all_to_all | solution.py:24
  73.8 0.1 reduce_sum.88
  73.9 0.6 slice_reduce_fusion
  74.5 0.0 copy-done.4
  75.2 0.0 copy-done.1
  75.2 0.9 %subtract_convert_fusion = (bf16[64,1280]{1,0:T(8,128)(2,1)}, f32[64,1280]{1,0:T(8,128)}) fusion(f32[64,1280]{1,0:T(8,128)S(1)} %copy-done.1, f32[]{:T(128)S(6)} %div.28, f32[1280]{0:T(1024)S(1)} %fusion.2, f32[64]{0:T(128)S(1)} %dynamic-slice_bitcast_fusion, f32[64,1280]{1,0:T(8,128)S(1)} %reduce_sum.82, f32[64,1280]{1,0:T(8,128)S(1)} %sub.6), kind=kLoop, calls=%fused_computation.2 | loop fusion | flops 655360 | bytes 1479940 | tf_op jit(solution)/shard_map/convert_element_type | solution.py:60
  76.1 0.0 copy-done.5
  76.1 0.0 copy-done.3
  (12 shorter events, 0.1 us)
Async XLA Ops:
  0.6 4.6 %copy-start = (f32[4,64,1280]{2,1,0:T(8,128)S(1)}, f32[4,64,1280]{2,1,0:T(8,128)}, u32[]{:S(2)}) copy-start(f32[4,64,1280]{2,1,0:T(8,128)} %param.10) | copy-start | bytes 3932164
  0.6 4.6 %copy-start.6 = (f32[4]{0:T(128)S(1)}, f32[4]{0:T(128)}, u32[]{:S(2)}) copy-start(f32[4]{0:T(128)} %param.12) | copy-start | bytes 52
  0.7 22.5 %all-to-all-start = ((f32[4,64,1280]{2,1,0:T(8,128)}), f32[4,64,1280]{2,1,0:T(8,128)S(1)}, u32[]{:S(2)}, u32[]{:S(2)}) async-start(f32[4,64,1280]{2,1,0:T(8,128)} %bitcast.7), calls=%async_computation | async-start | bytes 2621440 | tf_op jit(solution)/shard_map/all_to_all | solution.py:39
  5.3 1.0 %copy-start.2 = (f32[64,1280]{1,0:T(8,128)S(1)}, f32[64,1280]{1,0:T(8,128)}, u32[]{:S(2)}) copy-start(f32[64,1280]{1,0:T(8,128)} %param.9) | copy-start | bytes 983044
  5.3 1.0 %copy-start.7 = (f32[4]{0:T(128)S(1)}, f32[4]{0:T(128)}, u32[]{:S(2)}) copy-start(f32[4]{0:T(128)} %param.11) | copy-start | bytes 52
  7.5 15.9 %copy-start.8 = (f32[64]{0:T(128)S(1)}, f32[64]{0:T(128)}, u32[]{:S(2)}) copy-start(f32[64]{0:T(128)} %param.14) | copy-start | bytes 772
  7.5 67.0 %copy-start.4 = (f32[1280]{0:T(1024)S(1)}, f32[1280]{0:T(1024)}, u32[]{:S(2)}) copy-start(f32[1280]{0:T(1024)} %param.15) | copy-start | bytes 15364
  7.5 67.6 %copy-start.1 = (f32[64,1280]{1,0:T(8,128)S(1)}, f32[64,1280]{1,0:T(8,128)}, u32[]{:S(2)}) copy-start(f32[64,1280]{1,0:T(8,128)} %param.13) | copy-start | bytes 983044
  24.0 27.7 %all-to-all-start.1 = ((f32[32,1,64]{2,1,0:T(1,128)}), f32[32,1,64]{2,1,0:T(1,128)S(1)}, u32[]{:S(2)}, u32[]{:S(2)}) async-start(f32[32,1,64]{2,1,0:T(1,128)} %broadcast_in_dim.6), calls=%async_computation.1 | async-start | bytes 32768 | tf_op jit(solution)/shard_map/all_to_all | solution.py:24
  52.4 8.9 %all-to-all-start.2 = ((f32[4,1,1280]{2,1,0:T(1,128)}), f32[4,1,1280]{2,1,0:T(1,128)S(1)}, u32[]{:S(2)}, u32[]{:S(2)}) async-start(f32[4,1,1280]{2,1,0:T(1,128)} %broadcast_in_dim.7), calls=%async_computation.2 | async-start | bytes 40960 | tf_op jit(solution)/shard_map/all_to_all | solution.py:24
  62.0 11.9 %all-to-all-start.3 = ((f32[16,1,1344]{2,1,0:T(1,128)}), f32[16,1,1344]{2,1,0:T(1,128)S(1)}, u32[]{:S(2)}, u32[]{:S(2)}) async-start(f32[16,1,1344]{2,1,0:T(1,128)} %broadcast_in_dim.8), calls=%async_computation.3 | async-start | bytes 180224 | tf_op jit(solution)/shard_map/all_to_all | solution.py:24
  67.4 8.7 %copy-start.5 = (f32[64]{0:T(128)}, f32[64]{0:T(128)S(1)}, u32[]{:S(2)}) copy-start(f32[64]{0:T(128)S(1)} %dynamic-slice_bitcast_fusion) | copy-start | bytes 772
  74.5 1.6 %copy-start.3 = (f32[1280]{0:T(1024)}, f32[1280]{0:T(1024)S(1)}, u32[]{:S(2)}) copy-start(f32[1280]{0:T(1024)S(1)} %fusion.2) | copy-start | bytes 15364

commit v2 on v1

v2 whole, which is shorter than its diff:
```python
import jax
import jax.numpy as jnp
from jax import lax
from jax.sharding import Mesh
from jax.sharding import PartitionSpec as P

D = 4096
FF = 10240
NOISE_STD = 2.0
DECAY_RATE = 0.85
LEARN_RATE = 0.01
TINY_TERM = 1e-30

ROW = ("x", "zl")
COL = ("zh", "core")
RUN = ("zl", "core")
PLANE = ("dp", "x")


def sum_of_sent(messages, axes):
    arrived = lax.all_to_all(messages, axes, split_axis=0, concat_axis=0, tiled=True)
    return arrived.sum(axis=0)


def per_device(
    grad_parts,
    gauss_noise,
    blt_buffers,
    blt_decays,
    blt_weights,
    master_weights,
    row_stat,
    col_stat,
):
    rows, cols = gauss_noise.shape
    n_col, n_run, n_plane = (lax.axis_size(axes) for axes in (COL, RUN, PLANE))
    arrived = lax.all_to_all(
        grad_parts.reshape(-1, rows, cols), "dp", split_axis=0, concat_axis=0, tiled=True
    )
    correlated = gauss_noise - jnp.sum(blt_buffers * blt_weights[:, None, None], axis=0)
    new_buffers = blt_decays[:, None, None] * blt_buffers + correlated[None]
    to = jnp.arange(n_run)
    same_cols = (to % 2 == lax.axis_index("core")).astype(jnp.float32)
    same_rows = (to // 2 == lax.axis_index("zl")).astype(jnp.float32)
    takes = jnp.concatenate(
        [
            jnp.broadcast_to(same_cols[:, None], (n_run, cols)),
            jnp.ones((n_run, rows), jnp.float32),
            jnp.broadcast_to(same_rows[:, None], (n_run, rows)),
        ],
        axis=1,
    )
    ones = jnp.broadcast_to(same_cols[0] + same_cols[1], (rows, rows))
    arrived, correlated, new_buffers, takes, row_stat, ones = lax.optimization_barrier(
        (arrived, correlated, new_buffers, takes, row_stat, ones)
    )
    noisy = arrived.sum(axis=0) + NOISE_STD * correlated
    squares = noisy * noisy
    share = DECAY_RATE / n_col * row_stat + (1.0 - DECAY_RATE) * (
        jnp.sum(squares, axis=1) / FF + TINY_TERM / n_col
    )
    sums = jnp.concatenate([jnp.sum(squares, axis=0), share, share])
    sums, col_stat, master_weights, takes = lax.optimization_barrier(
        (sums, col_stat, master_weights, takes)
    )
    run = sum_of_sent(sums[None] * takes, RUN)
    run, own = lax.optimization_barrier((run, run[cols + rows :]))
    plane = sum_of_sent(jnp.broadcast_to(run[None], (n_plane, *run.shape)), PLANE)
    stats = jnp.concatenate([plane[cols : cols + rows], own])
    new_col = DECAY_RATE * col_stat + (1.0 - DECAY_RATE) * (plane[:cols] / D + TINY_TERM)
    stats, new_col = lax.optimization_barrier((stats, new_col))
    stats = lax.psum(stats, "zh")
    shares, new_row = lax.optimization_barrier((stats[:rows], stats[rows:]))
    row_mean = jnp.sum(ones * shares[None, :], axis=1) / D
    direction = noisy / jnp.sqrt((new_row / row_mean)[:, None] * new_col[None, :])
    weight_copy = (master_weights - LEARN_RATE * direction).astype(jnp.bfloat16)
    return (direction, weight_copy, new_buffers, new_row, new_col)


def solution(mesh):
    finer = Mesh(
        mesh.devices.reshape(mesh.shape["dp"], 4, 4, 4, 2),
        ("dp", "x", "zl", "zh", "core"),
    )
    rows = ("dp", *ROW)
    return jax.shard_map(
        per_device,
        mesh=finer,
        in_specs=(
            P("dp", None, ROW, COL),
            P(rows, COL),
            P(None, rows, COL),
            P(),
            P(),
            P(rows, COL),
            P(rows),
            P(COL),
        ),
        out_specs=(P(rows, COL), P(rows, COL), P(None, rows, COL), P(rows), P(COL)),
        check_vma=False,
    )
```

time: 76.5 us -> 67.1 us (0.88)
  blocking collectives: 0 us -> 41.7 us
  waiting for transfers between devices: 39.8 us -> 14.1 us
  starting transfers between devices: 28.8 us -> 4.61 us
  local copies, waits for them, and re-layouts: 2.76 us -> 1.35 us
    all_to_all x3 -> x0, starting transfers between devices: 24.2 us -> none  [from_all(): return lax.all_to_all(copies, axes, split_axis=0, concat_axis=0, tiled=True)]
    all_to_all x3 -> x0, waiting for transfers between devices: 24.1 us -> none  [from_all(): return lax.all_to_all(copies, axes, split_axis=0, concat_axis=0, tiled=True)]
    all_to_all x0 -> x2, blocking collectives: none -> 23.2 us  [sum_of_sent(): lax.all_to_all(messages, axes, split_axis=0, concat_axis=0, tiled=True)]
    psum x0 -> x1, blocking collectives: none -> 18.5 us  [per_device(): stats = lax.psum(stats, 'zh')]
    broadcast_in_dim x3 -> x5, local copies, waits for them, and re-layouts: 1.92 us -> 0.19 us  [the longest x1 0.07 us: per_device(): jnp.broadcast_to(same_cols[:, None], (n_run, cols))]
    all_to_all x1, waiting for transfers between devices: 15.6 us -> 14.1 us  [per_device(): lax.all_to_all(grad_parts.reshape(-1, rows, cols), 'dp', split_axis=0, co...]
  transfers between devices with their start and end apart: 4 -> 1, of which waited for: 4 -> 1; matrix products, arithmetic and copies ran while one was open for 2% -> 3% of each run, Pallas kernels for 0% -> 0%
where the time goes in v2:
time: 67.1 us; the launch traced here: 66.8 us
  blocking collectives  41.7 us (62%)
  waiting for transfers between devices  14.1 us (21%)
  starting transfers between devices  4.61 us (7%)
  other arithmetic  2.93 us (4%)
  between operations  2.1 us (3%)
  local copies, waits for them, and re-layouts  1.35 us (2%)
    all_to_all x2, blocking collectives, sum_of_sent(): lax.all_to_all(messages, axes, split_axis=0, concat_axis=0, tiled=True)  23.2 us
    psum x1, blocking collectives, per_device(): stats = lax.psum(stats, 'zh')  18.5 us
    all_to_all x1, waiting for transfers between devices, per_device(): lax.all_to_all(grad_parts.reshape(-1, rows, cols), 'dp', split_axis=0, co...  14.1 us
    all_to_all x1, starting transfers between devices, per_device(): lax.all_to_all(grad_parts.reshape(-1, rows, cols), 'dp', split_axis=0, co...  4.61 us
  transfers between devices with their start and end apart: 1, of which 1 were waited for; matrix products, arithmetic and copies ran while one was open for 3% of the time, Pallas kernels for 0%

profile of v2, /device:TPU:2, one launch (start us, length us, event | category | flops | bytes accessed | tf_op | source)
XLA Modules:
  0.0 66.8 jit_solution(16642398468333567956)
XLA Ops:
  0.6 0.0 copy-start
  0.6 0.0 copy-start.5
  0.7 4.6 %all-to-all-start = ((f32[4,64,1280]{2,1,0:T(8,128)}), f32[4,64,1280]{2,1,0:T(8,128)S(1)}, u32[]{:S(2)}, u32[]{:S(2)}) async-start(f32[4,64,1280]{2,1,0:T(8,128)} %bitcast.2), calls=%async_computation | async-start | bytes 2621440 | tf_op jit(solution)/shard_map/all_to_all | solution.py:37
  5.3 0.6 fusion.4
  7.2 0.0 copy-done
  7.2 0.0 copy-done.5
  7.2 0.0 copy-start.6
  7.2 0.2 multiply_reduce_fusion
  7.3 0.0 copy-done.1
  7.4 0.1 broadcast_in_dim.12
  7.5 0.1 broadcast_in_dim.10
  7.6 0.1 concatenate.9
  7.6 0.2 copy-done.6
  7.8 1.2 %multiply_add_fusion = f32[4,64,1280]{2,1,0:T(8,128)} fusion(f32[4,64,1280]{2,1,0:T(8,128)S(1)} %copy-done, f32[64,1280]{1,0:T(8,128)S(1)} %sub.10, f32[4]{0:T(128)S(1)} %copy-done.6), kind=kLoop, calls=%fused_computation | loop fusion | flops 655360 | bytes 2949136 | tf_op jit(solution)/shard_map/add | solution.py:41
  9.1 14.1 %all-to-all-done = f32[4,64,1280]{2,1,0:T(8,128)S(1)} async-done(((f32[4,64,1280]{2,1,0:T(8,128)}), f32[4,64,1280]{2,1,0:T(8,128)S(1)}, u32[]{:S(2)}, u32[]{:S(2)}) %all-to-all-start) | async-done | bytes 1310752 | tf_op jit(solution)/shard_map/all_to_all | solution.py:37
  23.2 0.1 reduce_sum.64
  23.3 0.2 multiply_reduce_fusion.1
  23.4 0.0 copy-done.8
  23.4 0.1 concatenate.10
  23.6 11.5 %all_to_all.20 = f32[8,1,1408]{2,1,0:T(1,128)S(1)} all-to-all(f32[8,1,1408]{2,1,0:T(1,128)S(1)} %all_to_all.14), channel_id=1, replica_groups=mesh['dp'=4,'x'=4,'zl'=4,'zh'=4,'core'=2] {'zl','core'}, dimensions={0} | all-to-all | bytes 90112 | tf_op jit(solution)/shard_map/all_to_all | solution.py:21
  35.1 0.1 slice.28
  35.2 11.7 %all_to_all.21 = f32[16,1,1408]{2,1,0:T(1,128)S(1)} all-to-all(f32[16,1,1408]{2,1,0:T(1,128)S(1)} %broadcast_in_dim.14), channel_id=1, replica_groups=mesh['dp'=4,'x'=4,'zl'=4,'zh'=4,'core'=2] {'dp','x'}, dimensions={0} | all-to-all | bytes 180224 | tf_op jit(solution)/shard_map/all_to_all | solution.py:21
  46.9 0.1 reduce_sum.68
  47.0 0.0 copy-done.4
  47.0 0.0 copy-start.3
  47.0 0.1 pad_maximum_fusion
  47.1 18.5 %psum.7 = f32[128]{0:T(128)S(1)} all-reduce(f32[128]{0:T(128)S(1)} %pad_maximum_fusion), channel_id=1, replica_groups=mesh['dp'=4,'x'=4,'zl'=4,'zh'=4,'core'=2] {'zh'}, use_global_device_ids=true, to_apply=%region_6.7 | all-reduce | flops 128 | bytes 1024 | tf_op jit(solution)/shard_map/psum | solution.py:72
  65.6 0.1 fusion.3
  65.7 0.1 multiply_reduce_fusion.3
  65.8 0.0 copy-done.2
  65.8 0.9 %subtract_convert_fusion = (bf16[64,1280]{1,0:T(8,128)(2,1)}, f32[64,1280]{1,0:T(8,128)}) fusion(f32[64,1280]{1,0:T(8,128)S(1)} %copy-done.2, f32[1280]{0:T(1024)S(1)} %fusion.2, f32[64]{0:T(128)S(1)} %multiply_divide_fusion, f32[64,1280]{1,0:T(8,128)S(1)} %reduce_sum.64, f32[64,1280]{1,0:T(8,128)S(1)} %sub.10), kind=kLoop, calls=%fused_computation.2 | loop fusion | flops 573440 | bytes 1479936 | tf_op jit(solution)/shard_map/convert_element_type | solution.py:76
  66.8 0.0 copy-done.3
  (19 shorter events, 0.2 us)
Async XLA Ops:
  0.6 6.5 %copy-start = (f32[4,64,1280]{2,1,0:T(8,128)S(1)}, f32[4,64,1280]{2,1,0:T(8,128)}, u32[]{:S(2)}) copy-start(f32[4,64,1280]{2,1,0:T(8,128)} %param.10) | copy-start | bytes 3932164
  0.6 6.5 %copy-start.5 = (f32[4]{0:T(128)S(1)}, f32[4]{0:T(128)}, u32[]{:S(2)}) copy-start(f32[4]{0:T(128)} %param.12) | copy-start | bytes 52
  0.7 22.5 %all-to-all-start = ((f32[4,64,1280]{2,1,0:T(8,128)}), f32[4,64,1280]{2,1,0:T(8,128)S(1)}, u32[]{:S(2)}, u32[]{:S(2)}) async-start(f32[4,64,1280]{2,1,0:T(8,128)} %bitcast.2), calls=%async_computation | async-start | bytes 2621440 | tf_op jit(solution)/shard_map/all_to_all | solution.py:37
  5.3 2.1 %copy-start.1 = (f32[64,1280]{1,0:T(8,128)S(1)}, f32[64,1280]{1,0:T(8,128)}, u32[]{:S(2)}) copy-start(f32[64,1280]{1,0:T(8,128)} %param.9) | copy-start | bytes 983044
  7.2 0.7 copy-start.6
  9.1 14.4 %copy-start.8 = (f32[64]{0:T(128)S(1)}, f32[64]{0:T(128)}, u32[]{:S(2)}) copy-start(f32[64]{0:T(128)} %param.14) | copy-start | bytes 772
  23.2 23.8 %copy-start.4 = (f32[1280]{0:T(1024)S(1)}, f32[1280]{0:T(1024)}, u32[]{:S(2)}) copy-start(f32[1280]{0:T(1024)} %param.15) | copy-start | bytes 15364
  23.2 42.7 %copy-start.2 = (f32[64,1280]{1,0:T(8,128)S(1)}, f32[64,1280]{1,0:T(8,128)}, u32[]{:S(2)}) copy-start(f32[64,1280]{1,0:T(8,128)} %param.13) | copy-start | bytes 983044
  47.0 19.8 %copy-start.3 = (f32[1280]{0:T(1024)}, f32[1280]{0:T(1024)S(1)}, u32[]{:S(2)}) copy-start(f32[1280]{0:T(1024)S(1)} %fusion.2) | copy-start | bytes 15364
  65.7 1.1 %copy-start.7 = (f32[64]{0:T(128)}, f32[64]{0:T(128)S(1)}, u32[]{:S(2)}) copy-start(f32[64]{0:T(128)S(1)} %get-tuple-element.19) | copy-start | bytes 772

commit v3 on v2

--- a/solution.py
+++ b/solution.py
@@ -3,6 +3,7 @@
 from jax import lax
 from jax.sharding import Mesh
 from jax.sharding import PartitionSpec as P
+
 
 D = 4096
 FF = 10240
@@ -20,6 +21,24 @@
 def sum_of_sent(messages, axes):
     arrived = lax.all_to_all(messages, axes, split_axis=0, concat_axis=0, tiled=True)
     return arrived.sum(axis=0)
+
+
+def sum_over_zh(mine, part_01, part_23, is_01, is_1, is_3):
+    def push(values, *pairs):
+        return lax.ppermute(values, "zh", pairs)
+
+    n = mine.shape[0]
+    again = lax.optimization_barrier(mine)
+    a = push(mine, (2, 0))
+    b = push(mine, (3, 0))
+    c = push(mine, (1, 0), (2, 1))
+    d = push(jnp.concatenate([mine, b]), (0, 1), (2, 3))
+    e = push(mine + c, (0, 3), (3, 2))
+    f = push(again + d[:n], (1, 2))
+    is_0, is_2 = is_01 - is_1, 1.0 - is_01 - is_3
+    from_01 = part_01 + is_0 * c + is_1 * d[:n] + is_3 * e + f
+    from_23 = part_23 + a + b + is_1 * c + d[n:] + is_3 * d[:n] + is_2 * e
+    return from_01 + from_23
 
 
 def per_device(
@@ -51,8 +70,12 @@
         axis=1,
     )
     ones = jnp.broadcast_to(same_cols[0] + same_cols[1], (rows, rows))
-    arrived, correlated, new_buffers, takes, row_stat, ones = lax.optimization_barrier(
-        (arrived, correlated, new_buffers, takes, row_stat, ones)
+    zh = lax.axis_index("zh")
+    is_01, is_1, is_3 = (
+        jnp.broadcast_to(here.astype(jnp.float32), (2 * rows,)) for here in (zh < 2, zh == 1, zh == 3)
+    )
+    arrived, correlated, new_buffers, takes, row_stat, ones, is_01, is_1, is_3 = lax.optimization_barrier(
+        (arrived, correlated, new_buffers, takes, row_stat, ones, is_01, is_1, is_3)
     )
     noisy = arrived.sum(axis=0) + NOISE_STD * correlated
     squares = noisy * noisy
@@ -68,8 +91,9 @@
     plane = sum_of_sent(jnp.broadcast_to(run[None], (n_plane, *run.shape)), PLANE)
     stats = jnp.concatenate([plane[cols : cols + rows], own])
     new_col = DECAY_RATE * col_stat + (1.0 - DECAY_RATE) * (plane[:cols] / D + TINY_TERM)
-    stats, new_col = lax.optimization_barrier((stats, new_col))
-    stats = lax.psum(stats, "zh")
+    part_01, part_23 = is_01 * stats, (1.0 - is_01) * stats
+    stats, new_col, part_01, part_23 = lax.optimization_barrier((stats, new_col, part_01, part_23))
+    stats = sum_over_zh(stats, part_01, part_23, is_01, is_1, is_3)
     shares, new_row = lax.optimization_barrier((stats[:rows], stats[rows:]))
     row_mean = jnp.sum(ones * shares[None, :], axis=1) / D
     direction = noisy / jnp.sqrt((new_row / row_mean)[:, None] * new_col[None, :])

time: 67.1 us -> 76.4 us (1.14)
  waiting for transfers between devices: 14.1 us -> 34.6 us
  blocking collectives: 41.7 us -> 23.2 us
  starting transfers between devices: 4.61 us -> 11.7 us
    ppermute x0 -> x6, waiting for transfers between devices: none -> 20.6 us  [push(): return lax.ppermute(values, 'zh', pairs)]
    psum x1 -> x0, blocking collectives: 18.5 us -> none  [per_device(): stats = lax.psum(stats, 'zh')]
    ppermute x0 -> x6, starting transfers between devices: none -> 7.08 us  [push(): return lax.ppermute(values, 'zh', pairs)]
  transfers between devices with their start and end apart: 1 -> 7, of which waited for: 1 -> 4; matrix products, arithmetic and copies ran while one was open for 3% -> 3% of each run, Pallas kernels for 0% -> 0%
where the time goes in v3:
time: 76.4 us; the launch traced here: 76 us
  waiting for transfers between devices  34.6 us (45%)
  blocking collectives  23.2 us (30%)
  starting transfers between devices  11.7 us (15%)
  other arithmetic  2.97 us (4%)
  between operations  2.2 us (3%)
  local copies, waits for them, and re-layouts  1.36 us (2%)
    all_to_all x2, blocking collectives, sum_of_sent(): lax.all_to_all(messages, axes, split_axis=0, concat_axis=0, tiled=True)  23.2 us
    ppermute x6, waiting for transfers between devices, push(): return lax.ppermute(values, 'zh', pairs)  20.6 us
    all_to_all x1, waiting for transfers between devices, per_device(): lax.all_to_all(grad_parts.reshape(-1, rows, cols), 'dp', split_axis=0, co...  14.1 us
    ppermute x6, starting transfers between devices, push(): return lax.ppermute(values, 'zh', pairs)  7.08 us
    all_to_all x1, starting transfers between devices, per_device(): lax.all_to_all(grad_parts.reshape(-1, rows, cols), 'dp', split_axis=0, co...  4.61 us
  transfers between devices with their start and end apart: 7, of which 4 were waited for; matrix products, arithmetic and copies ran while one was open for 3% of the time, Pallas kernels for 0%

profile of v3, /device:TPU:2, one launch (start us, length us, event | category | flops | bytes accessed | tf_op | source)
XLA Modules:
  0.0 76.0 jit_solution(11956057648248772916)
XLA Ops:
  0.7 4.6 %all-to-all-start = ((f32[4,64,1280]{2,1,0:T(8,128)}), f32[4,64,1280]{2,1,0:T(8,128)S(1)}, u32[]{:S(2)}, u32[]{:S(2)}) async-start(f32[4,64,1280]{2,1,0:T(8,128)} %bitcast.2), calls=%async_computation | async-start | bytes 2621440 | tf_op jit(solution)/shard_map/all_to_all | solution.py:56
  5.3 0.6 fusion.4
  7.2 0.0 copy-start.6
  7.2 0.2 multiply_reduce_fusion
  7.4 0.1 broadcast_in_dim.18
  7.5 0.1 broadcast_in_dim.16
  7.6 0.1 concatenate.12
  7.7 0.2 copy-done.6
  7.8 1.2 %multiply_add_fusion = f32[4,64,1280]{2,1,0:T(8,128)} fusion(f32[4,64,1280]{2,1,0:T(8,128)S(1)} %copy-done, f32[64,1280]{1,0:T(8,128)S(1)} %sub.20, f32[4]{0:T(128)S(1)} %copy-done.6), kind=kLoop, calls=%fused_computation | loop fusion | flops 655360 | bytes 2949136 | tf_op jit(solution)/shard_map/add | solution.py:60
  9.1 14.1 %all-to-all-done = f32[4,64,1280]{2,1,0:T(8,128)S(1)} async-done(((f32[4,64,1280]{2,1,0:T(8,128)}), f32[4,64,1280]{2,1,0:T(8,128)S(1)}, u32[]{:S(2)}, u32[]{:S(2)}) %all-to-all-start) | async-done | bytes 1310752 | tf_op jit(solution)/shard_map/all_to_all | solution.py:56
  23.2 0.0 copy-start.4
  23.2 0.0 copy-start.2
  23.2 0.1 reduce_sum.64
  23.3 0.2 multiply_reduce_fusion.1
  23.5 0.1 concatenate.13
  23.6 11.5 %all_to_all.20 = f32[8,1,1408]{2,1,0:T(1,128)S(1)} all-to-all(f32[8,1,1408]{2,1,0:T(1,128)S(1)} %all_to_all.14), channel_id=1, replica_groups=mesh['dp'=4,'x'=4,'zl'=4,'zh'=4,'core'=2] {'zl','core'}, dimensions={0} | all-to-all | bytes 90112 | tf_op jit(solution)/shard_map/all_to_all | solution.py:22
  35.1 0.1 slice.38
  35.3 11.7 %all_to_all.21 = f32[16,1,1408]{2,1,0:T(1,128)S(1)} all-to-all(f32[16,1,1408]{2,1,0:T(1,128)S(1)} %broadcast_in_dim.23), channel_id=1, replica_groups=mesh['dp'=4,'x'=4,'zl'=4,'zh'=4,'core'=2] {'dp','x'}, dimensions={0} | all-to-all | bytes 180224 | tf_op jit(solution)/shard_map/all_to_all | solution.py:22
  46.9 0.1 reduce_sum.68
  47.0 0.1 subtract_multiply_fusion
  47.1 1.3 %collective-permute-start.1 = (f32[128]{0:T(128)S(1)}, f32[128]{0:T(128)S(1)}, u32[]{:S(2)}, u32[]{:S(2)}) collective-permute-start(f32[128]{0:T(128)S(1)} %get-tuple-element.38), channel_id=1, source_target_pairs={{6,0},{7,1},{14,8},{15,9},{22,16},{23,17},{30,24},{31,25},{38,32},... | collective-permute-start | bytes 1544 | tf_op jit(solution)/shard_map/ppermute | solution.py:28
  48.4 9.7 %collective-permute-done.1 = f32[128]{0:T(128)S(1)} collective-permute-done((f32[128]{0:T(128)S(1)}, f32[128]{0:T(128)S(1)}, u32[]{:S(2)}, u32[]{:S(2)}) %collective-permute-start.1) | collective-permute-done | bytes 544 | tf_op jit(solution)/shard_map/ppermute | solution.py:28
  58.1 1.3 %collective-permute-start.2 = (f32[256]{0:T(256)S(1)}, f32[256]{0:T(256)S(1)}, u32[]{:S(2)}, u32[]{:S(2)}) collective-permute-start(f32[256]{0:T(256)S(1)} %pad_maximum_fusion), channel_id=1, source_target_pairs={{0,2},{4,6},{1,3},{5,7},{8,10},{12,14},{9,11},{13,15},{16,18},{20,... | collective-permute-start | bytes 3080 | tf_op jit(solution)/shard_map/ppermute | solution.py:28
  59.4 1.3 %collective-permute-start = (f32[128]{0:T(128)S(1)}, f32[128]{0:T(128)S(1)}, u32[]{:S(2)}, u32[]{:S(2)}) collective-permute-start(f32[128]{0:T(128)S(1)} %get-tuple-element.38), channel_id=1, source_target_pairs={{2,0},{4,2},{3,1},{5,3},{10,8},{12,10},{11,9},{13,11},{18,16},{20,... | collective-permute-start | bytes 1544 | tf_op jit(solution)/shard_map/ppermute | solution.py:28
  60.7 1.3 %collective-permute-start.5 = (f32[128]{0:T(128)S(1)}, f32[128]{0:T(128)S(1)}, u32[]{:S(2)}, u32[]{:S(2)}) collective-permute-start(f32[128]{0:T(128)S(1)} %get-tuple-element.38), channel_id=1, source_target_pairs={{4,0},{5,1},{12,8},{13,9},{20,16},{21,17},{28,24},{29,25},{36,32},... | collective-permute-start | bytes 1544 | tf_op jit(solution)/shard_map/ppermute | solution.py:28
  62.0 6.8 %collective-permute-done = f32[128]{0:T(128)S(1)} collective-permute-done((f32[128]{0:T(128)S(1)}, f32[128]{0:T(128)S(1)}, u32[]{:S(2)}, u32[]{:S(2)}) %collective-permute-start) | collective-permute-done | bytes 544 | tf_op jit(solution)/shard_map/ppermute | solution.py:28
  68.7 1.3 %collective-permute-start.3 = (f32[128]{0:T(128)S(1)}, f32[128]{0:T(128)S(1)}, u32[]{:S(2)}, u32[]{:S(2)}) collective-permute-start(f32[128]{0:T(128)S(1)} %add.103), channel_id=1, source_target_pairs={{0,6},{6,4},{1,7},{7,5},{8,14},{14,12},{9,15},{15,13},{16,22},{22,... | collective-permute-start | bytes 1544 | tf_op jit(solution)/shard_map/ppermute | solution.py:28
  70.0 0.7 collective-permute-start.4
  70.7 4.1 %collective-permute-done.5 = f32[128]{0:T(128)S(1)} collective-permute-done((f32[128]{0:T(128)S(1)}, f32[128]{0:T(128)S(1)}, u32[]{:S(2)}, u32[]{:S(2)}) %collective-permute-start.5) | collective-permute-done | bytes 544 | tf_op jit(solution)/shard_map/ppermute | solution.py:28
  74.9 0.1 fusion.3
  74.9 0.1 multiply_reduce_fusion.3
  75.1 0.9 %subtract_convert_fusion = (bf16[64,1280]{1,0:T(8,128)(2,1)}, f32[64,1280]{1,0:T(8,128)}) fusion(f32[64,1280]{1,0:T(8,128)S(1)} %copy-done.2, f32[1280]{0:T(1024)S(1)} %fusion.2, f32[64]{0:T(128)S(1)} %multiply_divide_fusion, f32[64,1280]{1,0:T(8,128)S(1)} %reduce_sum.64, f32[64,1280]{1,0:T(8,128)S(1)} %sub.20), kind=kLoop, calls=%fused_computation.2 | loop fusion | flops 573440 | bytes 1479936 | tf_op jit(solution)/shard_map/convert_element_type | solution.py:100
  (38 shorter events, 0.3 us)
Async XLA Ops:
  0.6 6.5 %copy-start = (f32[4,64,1280]{2,1,0:T(8,128)S(1)}, f32[4,64,1280]{2,1,0:T(8,128)}, u32[]{:S(2)}) copy-start(f32[4,64,1280]{2,1,0:T(8,128)} %param.10) | copy-start | bytes 3932164
  0.6 6.5 %copy-start.5 = (f32[4]{0:T(128)S(1)}, f32[4]{0:T(128)}, u32[]{:S(2)}) copy-start(f32[4]{0:T(128)} %param.12) | copy-start | bytes 52
  0.7 22.5 %all-to-all-start = ((f32[4,64,1280]{2,1,0:T(8,128)}), f32[4,64,1280]{2,1,0:T(8,128)S(1)}, u32[]{:S(2)}, u32[]{:S(2)}) async-start(f32[4,64,1280]{2,1,0:T(8,128)} %bitcast.2), calls=%async_computation | async-start | bytes 2621440 | tf_op jit(solution)/shard_map/all_to_all | solution.py:56
  5.3 2.1 %copy-start.1 = (f32[64,1280]{1,0:T(8,128)S(1)}, f32[64,1280]{1,0:T(8,128)}, u32[]{:S(2)}) copy-start(f32[64,1280]{1,0:T(8,128)} %param.9) | copy-start | bytes 983044
  7.2 0.7 copy-start.6
  9.1 14.4 %copy-start.8 = (f32[64]{0:T(128)S(1)}, f32[64]{0:T(128)}, u32[]{:S(2)}) copy-start(f32[64]{0:T(128)} %param.14) | copy-start | bytes 772
  23.2 23.8 %copy-start.4 = (f32[1280]{0:T(1024)S(1)}, f32[1280]{0:T(1024)}, u32[]{:S(2)}) copy-start(f32[1280]{0:T(1024)} %param.15) | copy-start | bytes 15364
  23.2 51.9 %copy-start.2 = (f32[64,1280]{1,0:T(8,128)S(1)}, f32[64,1280]{1,0:T(8,128)}, u32[]{:S(2)}) copy-start(f32[64,1280]{1,0:T(8,128)} %param.13) | copy-start | bytes 983044
  47.0 29.0 %copy-start.3 = (f32[1280]{0:T(1024)}, f32[1280]{0:T(1024)S(1)}, u32[]{:S(2)}) copy-start(f32[1280]{0:T(1024)S(1)} %fusion.2) | copy-start | bytes 15364
  47.1 10.9 %collective-permute-start.1 = (f32[128]{0:T(128)S(1)}, f32[128]{0:T(128)S(1)}, u32[]{:S(2)}, u32[]{:S(2)}) collective-permute-start(f32[128]{0:T(128)S(1)} %get-tuple-element.38), channel_id=1, source_target_pairs={{6,0},{7,1},{14,8},{15,9},{22,16},{23,17},{30,24},{31,25},{38,32},... | collective-permute-start | bytes 1544 | tf_op jit(solution)/shard_map/ppermute | solution.py:28
  58.1 11.9 %collective-permute-start.2 = (f32[256]{0:T(256)S(1)}, f32[256]{0:T(256)S(1)}, u32[]{:S(2)}, u32[]{:S(2)}) collective-permute-start(f32[256]{0:T(256)S(1)} %pad_maximum_fusion), channel_id=1, source_target_pairs={{0,2},{4,6},{1,3},{5,7},{8,10},{12,14},{9,11},{13,15},{16,18},{20,... | collective-permute-start | bytes 3080 | tf_op jit(solution)/shard_map/ppermute | solution.py:28
  59.4 9.4 %collective-permute-start = (f32[128]{0:T(128)S(1)}, f32[128]{0:T(128)S(1)}, u32[]{:S(2)}, u32[]{:S(2)}) collective-permute-start(f32[128]{0:T(128)S(1)} %get-tuple-element.38), channel_id=1, source_target_pairs={{2,0},{4,2},{3,1},{5,3},{10,8},{12,10},{11,9},{13,11},{18,16},{20,... | collective-permute-start | bytes 1544 | tf_op jit(solution)/shard_map/ppermute | solution.py:28
  60.7 14.2 %collective-permute-start.5 = (f32[128]{0:T(128)S(1)}, f32[128]{0:T(128)S(1)}, u32[]{:S(2)}, u32[]{:S(2)}) collective-permute-start(f32[128]{0:T(128)S(1)} %get-tuple-element.38), channel_id=1, source_target_pairs={{4,0},{5,1},{12,8},{13,9},{20,16},{21,17},{28,24},{29,25},{36,32},... | collective-permute-start | bytes 1544 | tf_op jit(solution)/shard_map/ppermute | solution.py:28
  68.7 6.1 %collective-permute-start.3 = (f32[128]{0:T(128)S(1)}, f32[128]{0:T(128)S(1)}, u32[]{:S(2)}, u32[]{:S(2)}) collective-permute-start(f32[128]{0:T(128)S(1)} %add.103), channel_id=1, source_target_pairs={{0,6},{6,4},{1,7},{7,5},{8,14},{14,12},{9,15},{15,13},{16,22},{22,... | collective-permute-start | bytes 1544 | tf_op jit(solution)/shard_map/ppermute | solution.py:28
  70.0 4.8 %collective-permute-start.4 = (f32[128]{0:T(128)S(1)}, f32[128]{0:T(128)S(1)}, u32[]{:S(2)}, u32[]{:S(2)}) collective-permute-start(f32[128]{0:T(128)S(1)} %slice_add_fusion), channel_id=1, source_target_pairs={{2,4},{3,5},{10,12},{11,13},{18,20},{19,21},{26,28},{27,29},{34,36... | collective-permute-start | bytes 1544 | tf_op jit(solution)/shard_map/ppermute | solution.py:28
  74.9 1.1 %copy-start.7 = (f32[64]{0:T(128)}, f32[64]{0:T(128)S(1)}, u32[]{:S(2)}) copy-start(f32[64]{0:T(128)S(1)} %get-tuple-element.24) | copy-start | bytes 772

commit v4 on v3

--- a/solution.py
+++ b/solution.py
@@ -33,11 +33,11 @@
     b = push(mine, (3, 0))
     c = push(mine, (1, 0), (2, 1))
     d = push(jnp.concatenate([mine, b]), (0, 1), (2, 3))
-    e = push(mine + c, (0, 3), (3, 2))
-    f = push(again + d[:n], (1, 2))
-    is_0, is_2 = is_01 - is_1, 1.0 - is_01 - is_3
-    from_01 = part_01 + is_0 * c + is_1 * d[:n] + is_3 * e + f
-    from_23 = part_23 + a + b + is_1 * c + d[n:] + is_3 * d[:n] + is_2 * e
+    e = push(mine + c, (0, 3))
+    f = push(jnp.concatenate([e, again]), (3, 2))
+    is_0 = is_01 - is_1
+    from_01 = part_01 + is_0 * c + is_1 * d[:n] + e + f[:n]
+    from_23 = part_23 + a + b + is_1 * c + d[n:] + is_3 * d[:n] + f[n:]
     return from_01 + from_23
 
 

time: 76.4 us -> 82.7 us (1.082)
  starting transfers between devices: 11.7 us -> 17.6 us
    ppermute x6, starting transfers between devices: 7.08 us -> 13 us  [push(): return lax.ppermute(values, 'zh', pairs)]
  transfers between devices with their start and end apart: 7 -> 7, of which waited for: 4 -> 3; matrix products, arithmetic and copies ran while one was open for 3% -> 3% of each run, Pallas kernels for 0% -> 0%
where the time goes in v4:
time: 82.7 us; the launch traced here: 82.3 us
  waiting for transfers between devices  35 us (42%)
  blocking collectives  23.2 us (28%)
  starting transfers between devices  17.6 us (21%)
  other arithmetic  2.97 us (4%)
  between operations  2.21 us (3%)
  local copies, waits for them, and re-layouts  1.36 us (2%)
    all_to_all x2, blocking collectives, sum_of_sent(): lax.all_to_all(messages, axes, split_axis=0, concat_axis=0, tiled=True)  23.2 us
    ppermute x6, waiting for transfers between devices, push(): return lax.ppermute(values, 'zh', pairs)  20.9 us
    all_to_all x1, waiting for transfers between devices, per_device(): lax.all_to_all(grad_parts.reshape(-1, rows, cols), 'dp', split_axis=0, co...  14.1 us
    ppermute x6, starting transfers between devices, push(): return lax.ppermute(values, 'zh', pairs)  13 us
    all_to_all x1, starting transfers between devices, per_device(): lax.all_to_all(grad_parts.reshape(-1, rows, cols), 'dp', split_axis=0, co...  4.61 us
  transfers between devices with their start and end apart: 7, of which 3 were waited for; matrix products, arithmetic and copies ran while one was open for 3% of the time, Pallas kernels for 0%

profile of v4, /device:TPU:2, one launch (start us, length us, event | category | flops | bytes accessed | tf_op | source)
XLA Modules:
  0.0 82.3 jit_solution(7903370263767684971)
XLA Ops:
  0.7 4.6 %all-to-all-start = ((f32[4,64,1280]{2,1,0:T(8,128)}), f32[4,64,1280]{2,1,0:T(8,128)S(1)}, u32[]{:S(2)}, u32[]{:S(2)}) async-start(f32[4,64,1280]{2,1,0:T(8,128)} %bitcast.2), calls=%async_computation | async-start | bytes 2621440 | tf_op jit(solution)/shard_map/all_to_all | solution.py:56
  5.3 0.6 fusion.4
  7.2 0.0 copy-start.6
  7.2 0.2 multiply_reduce_fusion
  7.4 0.1 broadcast_in_dim.18
  7.5 0.1 broadcast_in_dim.16
  7.6 0.1 concatenate.15
  7.7 0.2 copy-done.6
  7.8 1.2 %multiply_add_fusion = f32[4,64,1280]{2,1,0:T(8,128)} fusion(f32[4,64,1280]{2,1,0:T(8,128)S(1)} %copy-done, f32[64,1280]{1,0:T(8,128)S(1)} %sub.19, f32[4]{0:T(128)S(1)} %copy-done.6), kind=kLoop, calls=%fused_computation | loop fusion | flops 655360 | bytes 2949136 | tf_op jit(solution)/shard_map/add | solution.py:60
  9.1 14.1 %all-to-all-done = f32[4,64,1280]{2,1,0:T(8,128)S(1)} async-done(((f32[4,64,1280]{2,1,0:T(8,128)}), f32[4,64,1280]{2,1,0:T(8,128)S(1)}, u32[]{:S(2)}, u32[]{:S(2)}) %all-to-all-start) | async-done | bytes 1310752 | tf_op jit(solution)/shard_map/all_to_all | solution.py:56
  23.2 0.0 copy-start.4
  23.2 0.0 copy-start.2
  23.2 0.1 reduce_sum.64
  23.3 0.2 multiply_reduce_fusion.1
  23.5 0.1 concatenate.16
  23.6 11.5 %all_to_all.20 = f32[8,1,1408]{2,1,0:T(1,128)S(1)} all-to-all(f32[8,1,1408]{2,1,0:T(1,128)S(1)} %all_to_all.14), channel_id=1, replica_groups=mesh['dp'=4,'x'=4,'zl'=4,'zh'=4,'core'=2] {'zl','core'}, dimensions={0} | all-to-all | bytes 90112 | tf_op jit(solution)/shard_map/all_to_all | solution.py:22
  35.1 0.1 slice.45
  35.3 11.7 %all_to_all.21 = f32[16,1,1408]{2,1,0:T(1,128)S(1)} all-to-all(f32[16,1,1408]{2,1,0:T(1,128)S(1)} %broadcast_in_dim.23), channel_id=1, replica_groups=mesh['dp'=4,'x'=4,'zl'=4,'zh'=4,'core'=2] {'dp','x'}, dimensions={0} | all-to-all | bytes 180224 | tf_op jit(solution)/shard_map/all_to_all | solution.py:22
  46.9 0.1 reduce_sum.68
  47.0 0.0 copy-start.3
  47.0 0.1 subtract_multiply_fusion
  47.1 1.3 %collective-permute-start = (f32[128]{0:T(128)S(1)}, f32[128]{0:T(128)S(1)}, u32[]{:S(2)}, u32[]{:S(2)}) collective-permute-start(f32[128]{0:T(128)S(1)} %get-tuple-element.38), channel_id=1, source_target_pairs={{2,0},{4,2},{3,1},{5,3},{10,8},{12,10},{11,9},{13,11},{18,16},{20,... | collective-permute-start | bytes 1544 | tf_op jit(solution)/shard_map/ppermute | solution.py:28
  48.4 1.3 %collective-permute-start.1 = (f32[128]{0:T(128)S(1)}, f32[128]{0:T(128)S(1)}, u32[]{:S(2)}, u32[]{:S(2)}) collective-permute-start(f32[128]{0:T(128)S(1)} %get-tuple-element.38), channel_id=1, source_target_pairs={{6,0},{7,1},{14,8},{15,9},{22,16},{23,17},{30,24},{31,25},{38,32},... | collective-permute-start | bytes 1544 | tf_op jit(solution)/shard_map/ppermute | solution.py:28
  49.7 8.0 %collective-permute-done = f32[128]{0:T(128)S(1)} collective-permute-done((f32[128]{0:T(128)S(1)}, f32[128]{0:T(128)S(1)}, u32[]{:S(2)}, u32[]{:S(2)}) %collective-permute-start) | collective-permute-done | bytes 544 | tf_op jit(solution)/shard_map/ppermute | solution.py:28
  57.7 1.4 %collective-permute-start.3 = (f32[128]{0:T(128)S(1)}, f32[128]{0:T(128)S(1)}, u32[]{:S(2)}, u32[]{:S(2)}) collective-permute-start(f32[128]{0:T(128)S(1)} %add.100), channel_id=1, source_target_pairs={{0,6},{1,7},{8,14},{9,15},{16,22},{17,23},{24,30},{25,31},{32,38},... | collective-permute-start | bytes 1544 | tf_op jit(solution)/shard_map/ppermute | solution.py:28
  59.2 7.1 %collective-permute-start.2 = (f32[256]{0:T(256)S(1)}, f32[256]{0:T(256)S(1)}, u32[]{:S(2)}, u32[]{:S(2)}) collective-permute-start(f32[256]{0:T(256)S(1)} %pad_maximum_fusion), channel_id=1, source_target_pairs={{0,2},{4,6},{1,3},{5,7},{8,10},{12,14},{9,11},{13,15},{16,18},{20,... | collective-permute-start | bytes 3080 | tf_op jit(solution)/shard_map/ppermute | solution.py:28
  66.3 0.7 collective-permute-start.4
  67.0 1.3 %collective-permute-start.5 = (f32[128]{0:T(128)S(1)}, f32[128]{0:T(128)S(1)}, u32[]{:S(2)}, u32[]{:S(2)}) collective-permute-start(f32[128]{0:T(128)S(1)} %get-tuple-element.38), channel_id=1, source_target_pairs={{4,0},{5,1},{12,8},{13,9},{20,16},{21,17},{28,24},{29,25},{36,32},... | collective-permute-start | bytes 1544 | tf_op jit(solution)/shard_map/ppermute | solution.py:28
  68.3 12.9 %collective-permute-done.5 = f32[128]{0:T(128)S(1)} collective-permute-done((f32[128]{0:T(128)S(1)}, f32[128]{0:T(128)S(1)}, u32[]{:S(2)}, u32[]{:S(2)}) %collective-permute-start.5) | collective-permute-done | bytes 544 | tf_op jit(solution)/shard_map/ppermute | solution.py:28
  81.2 0.1 fusion.3
  81.2 0.1 multiply_reduce_fusion.3
  81.4 0.9 %subtract_convert_fusion = (bf16[64,1280]{1,0:T(8,128)(2,1)}, f32[64,1280]{1,0:T(8,128)}) fusion(f32[64,1280]{1,0:T(8,128)S(1)} %copy-done.2, f32[1280]{0:T(1024)S(1)} %fusion.2, f32[64]{0:T(128)S(1)} %multiply_divide_fusion, f32[64,1280]{1,0:T(8,128)S(1)} %reduce_sum.64, f32[64,1280]{1,0:T(8,128)S(1)} %sub.19), kind=kLoop, calls=%fused_computation.2 | loop fusion | flops 573440 | bytes 1479936 | tf_op jit(solution)/shard_map/convert_element_type | solution.py:100
  (38 shorter events, 0.3 us)
Async XLA Ops:
  0.6 6.5 %copy-start = (f32[4,64,1280]{2,1,0:T(8,128)S(1)}, f32[4,64,1280]{2,1,0:T(8,128)}, u32[]{:S(2)}) copy-start(f32[4,64,1280]{2,1,0:T(8,128)} %param.10) | copy-start | bytes 3932164
  0.6 6.5 %copy-start.5 = (f32[4]{0:T(128)S(1)}, f32[4]{0:T(128)}, u32[]{:S(2)}) copy-start(f32[4]{0:T(128)} %param.12) | copy-start | bytes 52
  0.7 22.5 %all-to-all-start = ((f32[4,64,1280]{2,1,0:T(8,128)}), f32[4,64,1280]{2,1,0:T(8,128)S(1)}, u32[]{:S(2)}, u32[]{:S(2)}) async-start(f32[4,64,1280]{2,1,0:T(8,128)} %bitcast.2), calls=%async_computation | async-start | bytes 2621440 | tf_op jit(solution)/shard_map/all_to_all | solution.py:56
  5.3 2.1 %copy-start.1 = (f32[64,1280]{1,0:T(8,128)S(1)}, f32[64,1280]{1,0:T(8,128)}, u32[]{:S(2)}) copy-start(f32[64,1280]{1,0:T(8,128)} %param.9) | copy-start | bytes 983044
  7.2 0.7 copy-start.6
  9.1 14.4 %copy-start.8 = (f32[64]{0:T(128)S(1)}, f32[64]{0:T(128)}, u32[]{:S(2)}) copy-start(f32[64]{0:T(128)} %param.14) | copy-start | bytes 772
  23.2 23.8 %copy-start.4 = (f32[1280]{0:T(1024)S(1)}, f32[1280]{0:T(1024)}, u32[]{:S(2)}) copy-start(f32[1280]{0:T(1024)} %param.15) | copy-start | bytes 15364
  23.2 58.2 %copy-start.2 = (f32[64,1280]{1,0:T(8,128)S(1)}, f32[64,1280]{1,0:T(8,128)}, u32[]{:S(2)}) copy-start(f32[64,1280]{1,0:T(8,128)} %param.13) | copy-start | bytes 983044
  47.0 35.3 %copy-start.3 = (f32[1280]{0:T(1024)}, f32[1280]{0:T(1024)S(1)}, u32[]{:S(2)}) copy-start(f32[1280]{0:T(1024)S(1)} %fusion.2) | copy-start | bytes 15364
  47.1 10.6 %collective-permute-start = (f32[128]{0:T(128)S(1)}, f32[128]{0:T(128)S(1)}, u32[]{:S(2)}, u32[]{:S(2)}) collective-permute-start(f32[128]{0:T(128)S(1)} %get-tuple-element.38), channel_id=1, source_target_pairs={{2,0},{4,2},{3,1},{5,3},{10,8},{12,10},{11,9},{13,11},{18,16},{20,... | collective-permute-start | bytes 1544 | tf_op jit(solution)/shard_map/ppermute | solution.py:28
  48.4 10.7 %collective-permute-start.1 = (f32[128]{0:T(128)S(1)}, f32[128]{0:T(128)S(1)}, u32[]{:S(2)}, u32[]{:S(2)}) collective-permute-start(f32[128]{0:T(128)S(1)} %get-tuple-element.38), channel_id=1, source_target_pairs={{6,0},{7,1},{14,8},{15,9},{22,16},{23,17},{30,24},{31,25},{38,32},... | collective-permute-start | bytes 1544 | tf_op jit(solution)/shard_map/ppermute | solution.py:28
  57.7 8.5 %collective-permute-start.3 = (f32[128]{0:T(128)S(1)}, f32[128]{0:T(128)S(1)}, u32[]{:S(2)}, u32[]{:S(2)}) collective-permute-start(f32[128]{0:T(128)S(1)} %add.100), channel_id=1, source_target_pairs={{0,6},{1,7},{8,14},{9,15},{16,22},{17,23},{24,30},{25,31},{32,38},... | collective-permute-start | bytes 1544 | tf_op jit(solution)/shard_map/ppermute | solution.py:28
  59.2 22.0 %collective-permute-start.2 = (f32[256]{0:T(256)S(1)}, f32[256]{0:T(256)S(1)}, u32[]{:S(2)}, u32[]{:S(2)}) collective-permute-start(f32[256]{0:T(256)S(1)} %pad_maximum_fusion), channel_id=1, source_target_pairs={{0,2},{4,6},{1,3},{5,7},{8,10},{12,14},{9,11},{13,15},{16,18},{20,... | collective-permute-start | bytes 3080 | tf_op jit(solution)/shard_map/ppermute | solution.py:28
  66.3 14.9 %collective-permute-start.4 = (f32[256]{0:T(256)S(1)}, f32[256]{0:T(256)S(1)}, u32[]{:S(2)}, u32[]{:S(2)}) collective-permute-start(f32[256]{0:T(256)S(1)} %pad_maximum_fusion.1), channel_id=1, source_target_pairs={{6,4},{7,5},{14,12},{15,13},{22,20},{23,21},{30,28},{31,29},{38,36... | collective-permute-start | bytes 3080 | tf_op jit(solution)/shard_map/ppermute | solution.py:28
  67.0 14.2 %collective-permute-start.5 = (f32[128]{0:T(128)S(1)}, f32[128]{0:T(128)S(1)}, u32[]{:S(2)}, u32[]{:S(2)}) collective-permute-start(f32[128]{0:T(128)S(1)} %get-tuple-element.38), channel_id=1, source_target_pairs={{4,0},{5,1},{12,8},{13,9},{20,16},{21,17},{28,24},{29,25},{36,32},... | collective-permute-start | bytes 1544 | tf_op jit(solution)/shard_map/ppermute | solution.py:28
  81.2 1.1 %copy-start.7 = (f32[64]{0:T(128)}, f32[64]{0:T(128)S(1)}, u32[]{:S(2)}) copy-start(f32[64]{0:T(128)S(1)} %get-tuple-element.24) | copy-start | bytes 772

commit v5 on v4

--- a/solution.py
+++ b/solution.py
@@ -23,7 +23,7 @@
     return arrived.sum(axis=0)
 
 
-def sum_over_zh(mine, part_01, part_23, is_01, is_1, is_3):
+def sum_over_zh(mine, part_01, part_23, is_1, is_3):
     def push(values, *pairs):
         return lax.ppermute(values, "zh", pairs)
 
@@ -31,13 +31,12 @@
     again = lax.optimization_barrier(mine)
     a = push(mine, (2, 0))
     b = push(mine, (3, 0))
-    c = push(mine, (1, 0), (2, 1))
+    c = push(mine, (1, 0))
+    e = push(mine + c, (0, 3), (2, 1))
     d = push(jnp.concatenate([mine, b]), (0, 1), (2, 3))
-    e = push(mine + c, (0, 3))
     f = push(jnp.concatenate([e, again]), (3, 2))
-    is_0 = is_01 - is_1
-    from_01 = part_01 + is_0 * c + is_1 * d[:n] + e + f[:n]
-    from_23 = part_23 + a + b + is_1 * c + d[n:] + is_3 * d[:n] + f[n:]
+    from_01 = part_01 + c + is_1 * d[:n] + is_3 * e + f[:n]
+    from_23 = part_23 + a + b + is_1 * e + d[n:] + is_3 * d[:n] + f[n:]
     return from_01 + from_23
 
 
@@ -93,7 +92,7 @@
     new_col = DECAY_RATE * col_stat + (1.0 - DECAY_RATE) * (plane[:cols] / D + TINY_TERM)
     part_01, part_23 = is_01 * stats, (1.0 - is_01) * stats
     stats, new_col, part_01, part_23 = lax.optimization_barrier((stats, new_col, part_01, part_23))
-    stats = sum_over_zh(stats, part_01, part_23, is_01, is_1, is_3)
+    stats = sum_over_zh(stats, part_01, part_23, is_1, is_3)
     shares, new_row = lax.optimization_barrier((stats[:rows], stats[rows:]))
     row_mean = jnp.sum(ones * shares[None, :], axis=1) / D
     direction = noisy / jnp.sqrt((new_row / row_mean)[:, None] * new_col[None, :])

time: 82.7 us -> 76.9 us (0.930)
  starting transfers between devices: 17.6 us -> 12.4 us
    ppermute x6, starting transfers between devices: 13 us -> 7.82 us  [push(): return lax.ppermute(values, 'zh', pairs)]
where the time goes in v5:
time: 76.9 us; the launch traced here: 76.5 us
  waiting for transfers between devices  34.4 us (45%)
  blocking collectives  23.2 us (30%)
  starting transfers between devices  12.4 us (16%)
  other arithmetic  2.97 us (4%)
  between operations  2.21 us (3%)
  local copies, waits for them, and re-layouts  1.36 us (2%)
    all_to_all x2, blocking collectives, sum_of_sent(): lax.all_to_all(messages, axes, split_axis=0, concat_axis=0, tiled=True)  23.2 us
    ppermute x6, waiting for transfers between devices, push(): return lax.ppermute(values, 'zh', pairs)  20.3 us
    all_to_all x1, waiting for transfers between devices, per_device(): lax.all_to_all(grad_parts.reshape(-1, rows, cols), 'dp', split_axis=0, co...  14.1 us
    ppermute x6, starting transfers between devices, push(): return lax.ppermute(values, 'zh', pairs)  7.82 us
    all_to_all x1, starting transfers between devices, per_device(): lax.all_to_all(grad_parts.reshape(-1, rows, cols), 'dp', split_axis=0, co...  4.61 us
  transfers between devices with their start and end apart: 7, of which 3 were waited for; matrix products, arithmetic and copies ran while one was open for 3% of the time, Pallas kernels for 0%

profile of v5, /device:TPU:2, one launch (start us, length us, event | category | flops | bytes accessed | tf_op | source)
XLA Modules:
  0.0 76.5 jit_solution(5087285667425015218)
XLA Ops:
  0.7 4.6 %all-to-all-start = ((f32[4,64,1280]{2,1,0:T(8,128)}), f32[4,64,1280]{2,1,0:T(8,128)S(1)}, u32[]{:S(2)}, u32[]{:S(2)}) async-start(f32[4,64,1280]{2,1,0:T(8,128)} %bitcast.2), calls=%async_computation | async-start | bytes 2621440 | tf_op jit(solution)/shard_map/all_to_all | solution.py:55
  5.3 0.6 fusion.4
  7.2 0.0 copy-start.6
  7.2 0.2 multiply_reduce_fusion
  7.4 0.1 broadcast_in_dim.18
  7.5 0.1 broadcast_in_dim.16
  7.6 0.1 concatenate.15
  7.7 0.2 copy-done.6
  7.8 1.2 %multiply_add_fusion = f32[4,64,1280]{2,1,0:T(8,128)} fusion(f32[4,64,1280]{2,1,0:T(8,128)S(1)} %copy-done, f32[64,1280]{1,0:T(8,128)S(1)} %sub.16, f32[4]{0:T(128)S(1)} %copy-done.6), kind=kLoop, calls=%fused_computation | loop fusion | flops 655360 | bytes 2949136 | tf_op jit(solution)/shard_map/add | solution.py:59
  9.1 14.1 %all-to-all-done = f32[4,64,1280]{2,1,0:T(8,128)S(1)} async-done(((f32[4,64,1280]{2,1,0:T(8,128)}), f32[4,64,1280]{2,1,0:T(8,128)S(1)}, u32[]{:S(2)}, u32[]{:S(2)}) %all-to-all-start) | async-done | bytes 1310752 | tf_op jit(solution)/shard_map/all_to_all | solution.py:55
  23.2 0.0 copy-start.4
  23.2 0.0 copy-start.2
  23.2 0.1 reduce_sum.64
  23.3 0.2 multiply_reduce_fusion.1
  23.5 0.1 concatenate.16
  23.6 11.5 %all_to_all.20 = f32[8,1,1408]{2,1,0:T(1,128)S(1)} all-to-all(f32[8,1,1408]{2,1,0:T(1,128)S(1)} %all_to_all.14), channel_id=1, replica_groups=mesh['dp'=4,'x'=4,'zl'=4,'zh'=4,'core'=2] {'zl','core'}, dimensions={0} | all-to-all | bytes 90112 | tf_op jit(solution)/shard_map/all_to_all | solution.py:22
  35.1 0.1 slice.45
  35.3 11.7 %all_to_all.21 = f32[16,1,1408]{2,1,0:T(1,128)S(1)} all-to-all(f32[16,1,1408]{2,1,0:T(1,128)S(1)} %broadcast_in_dim.23), channel_id=1, replica_groups=mesh['dp'=4,'x'=4,'zl'=4,'zh'=4,'core'=2] {'dp','x'}, dimensions={0} | all-to-all | bytes 180224 | tf_op jit(solution)/shard_map/all_to_all | solution.py:22
  46.9 0.1 reduce_sum.68
  47.0 0.0 copy-start.3
  47.0 0.1 subtract_multiply_fusion
  47.1 1.3 %collective-permute-start = (f32[128]{0:T(128)S(1)}, f32[128]{0:T(128)S(1)}, u32[]{:S(2)}, u32[]{:S(2)}) collective-permute-start(f32[128]{0:T(128)S(1)} %get-tuple-element.37), channel_id=1, source_target_pairs={{2,0},{3,1},{10,8},{11,9},{18,16},{19,17},{26,24},{27,25},{34,32},... | collective-permute-start | bytes 1544 | tf_op jit(solution)/shard_map/ppermute | solution.py:28
  48.4 1.3 %collective-permute-start.1 = (f32[128]{0:T(128)S(1)}, f32[128]{0:T(128)S(1)}, u32[]{:S(2)}, u32[]{:S(2)}) collective-permute-start(f32[128]{0:T(128)S(1)} %get-tuple-element.37), channel_id=1, source_target_pairs={{6,0},{7,1},{14,8},{15,9},{22,16},{23,17},{30,24},{31,25},{38,32},... | collective-permute-start | bytes 1544 | tf_op jit(solution)/shard_map/ppermute | solution.py:28
  49.7 7.4 %collective-permute-done = f32[128]{0:T(128)S(1)} collective-permute-done((f32[128]{0:T(128)S(1)}, f32[128]{0:T(128)S(1)}, u32[]{:S(2)}, u32[]{:S(2)}) %collective-permute-start) | collective-permute-done | bytes 544 | tf_op jit(solution)/shard_map/ppermute | solution.py:28
  57.1 2.0 %collective-permute-start.3 = (f32[128]{0:T(128)S(1)}, f32[128]{0:T(128)S(1)}, u32[]{:S(2)}, u32[]{:S(2)}) collective-permute-start(f32[128]{0:T(128)S(1)} %add.100), channel_id=1, source_target_pairs={{0,6},{4,2},{1,7},{5,3},{8,14},{12,10},{9,15},{13,11},{16,22},{20,... | collective-permute-start | bytes 1544 | tf_op jit(solution)/shard_map/ppermute | solution.py:28
  59.2 1.3 %collective-permute-start.2 = (f32[256]{0:T(256)S(1)}, f32[256]{0:T(256)S(1)}, u32[]{:S(2)}, u32[]{:S(2)}) collective-permute-start(f32[256]{0:T(256)S(1)} %pad_maximum_fusion), channel_id=1, source_target_pairs={{0,2},{4,6},{1,3},{5,7},{8,10},{12,14},{9,11},{13,15},{16,18},{20,... | collective-permute-start | bytes 3080 | tf_op jit(solution)/shard_map/ppermute | solution.py:28
  60.5 0.7 collective-permute-start.4
  61.2 1.3 %collective-permute-start.5 = (f32[128]{0:T(128)S(1)}, f32[128]{0:T(128)S(1)}, u32[]{:S(2)}, u32[]{:S(2)}) collective-permute-start(f32[128]{0:T(128)S(1)} %get-tuple-element.37), channel_id=1, source_target_pairs={{4,0},{5,1},{12,8},{13,9},{20,16},{21,17},{28,24},{29,25},{36,32},... | collective-permute-start | bytes 1544 | tf_op jit(solution)/shard_map/ppermute | solution.py:28
  62.5 12.9 %collective-permute-done.5 = f32[128]{0:T(128)S(1)} collective-permute-done((f32[128]{0:T(128)S(1)}, f32[128]{0:T(128)S(1)}, u32[]{:S(2)}, u32[]{:S(2)}) %collective-permute-start.5) | collective-permute-done | bytes 544 | tf_op jit(solution)/shard_map/ppermute | solution.py:28
  75.4 0.1 fusion.3
  75.4 0.1 multiply_reduce_fusion.3
  75.6 0.9 %subtract_convert_fusion = (bf16[64,1280]{1,0:T(8,128)(2,1)}, f32[64,1280]{1,0:T(8,128)}) fusion(f32[64,1280]{1,0:T(8,128)S(1)} %copy-done.2, f32[1280]{0:T(1024)S(1)} %fusion.2, f32[64]{0:T(128)S(1)} %multiply_divide_fusion, f32[64,1280]{1,0:T(8,128)S(1)} %reduce_sum.64, f32[64,1280]{1,0:T(8,128)S(1)} %sub.16), kind=kLoop, calls=%fused_computation.2 | loop fusion | flops 573440 | bytes 1479936 | tf_op jit(solution)/shard_map/convert_element_type | solution.py:99
  (38 shorter events, 0.3 us)
Async XLA Ops:
  0.6 6.5 %copy-start = (f32[4,64,1280]{2,1,0:T(8,128)S(1)}, f32[4,64,1280]{2,1,0:T(8,128)}, u32[]{:S(2)}) copy-start(f32[4,64,1280]{2,1,0:T(8,128)} %param.10) | copy-start | bytes 3932164
  0.6 6.5 %copy-start.5 = (f32[4]{0:T(128)S(1)}, f32[4]{0:T(128)}, u32[]{:S(2)}) copy-start(f32[4]{0:T(128)} %param.12) | copy-start | bytes 52
  0.7 22.5 %all-to-all-start = ((f32[4,64,1280]{2,1,0:T(8,128)}), f32[4,64,1280]{2,1,0:T(8,128)S(1)}, u32[]{:S(2)}, u32[]{:S(2)}) async-start(f32[4,64,1280]{2,1,0:T(8,128)} %bitcast.2), calls=%async_computation | async-start | bytes 2621440 | tf_op jit(solution)/shard_map/all_to_all | solution.py:55
  5.3 2.1 %copy-start.1 = (f32[64,1280]{1,0:T(8,128)S(1)}, f32[64,1280]{1,0:T(8,128)}, u32[]{:S(2)}) copy-start(f32[64,1280]{1,0:T(8,128)} %param.9) | copy-start | bytes 983044
  7.2 0.7 copy-start.6
  9.1 14.4 %copy-start.8 = (f32[64]{0:T(128)S(1)}, f32[64]{0:T(128)}, u32[]{:S(2)}) copy-start(f32[64]{0:T(128)} %param.14) | copy-start | bytes 772
  23.2 23.8 %copy-start.4 = (f32[1280]{0:T(1024)S(1)}, f32[1280]{0:T(1024)}, u32[]{:S(2)}) copy-start(f32[1280]{0:T(1024)} %param.15) | copy-start | bytes 15364
  23.2 52.4 %copy-start.2 = (f32[64,1280]{1,0:T(8,128)S(1)}, f32[64,1280]{1,0:T(8,128)}, u32[]{:S(2)}) copy-start(f32[64,1280]{1,0:T(8,128)} %param.13) | copy-start | bytes 983044
  47.0 29.5 %copy-start.3 = (f32[1280]{0:T(1024)}, f32[1280]{0:T(1024)S(1)}, u32[]{:S(2)}) copy-start(f32[1280]{0:T(1024)S(1)} %fusion.2) | copy-start | bytes 15364
  47.1 10.0 %collective-permute-start = (f32[128]{0:T(128)S(1)}, f32[128]{0:T(128)S(1)}, u32[]{:S(2)}, u32[]{:S(2)}) collective-permute-start(f32[128]{0:T(128)S(1)} %get-tuple-element.37), channel_id=1, source_target_pairs={{2,0},{3,1},{10,8},{11,9},{18,16},{19,17},{26,24},{27,25},{34,32},... | collective-permute-start | bytes 1544 | tf_op jit(solution)/shard_map/ppermute | solution.py:28
  48.4 10.7 %collective-permute-start.1 = (f32[128]{0:T(128)S(1)}, f32[128]{0:T(128)S(1)}, u32[]{:S(2)}, u32[]{:S(2)}) collective-permute-start(f32[128]{0:T(128)S(1)} %get-tuple-element.37), channel_id=1, source_target_pairs={{6,0},{7,1},{14,8},{15,9},{22,16},{23,17},{30,24},{31,25},{38,32},... | collective-permute-start | bytes 1544 | tf_op jit(solution)/shard_map/ppermute | solution.py:28
  57.1 3.3 %collective-permute-start.3 = (f32[128]{0:T(128)S(1)}, f32[128]{0:T(128)S(1)}, u32[]{:S(2)}, u32[]{:S(2)}) collective-permute-start(f32[128]{0:T(128)S(1)} %add.100), channel_id=1, source_target_pairs={{0,6},{4,2},{1,7},{5,3},{8,14},{12,10},{9,15},{13,11},{16,22},{20,... | collective-permute-start | bytes 1544 | tf_op jit(solution)/shard_map/ppermute | solution.py:28
  59.2 16.2 %collective-permute-start.2 = (f32[256]{0:T(256)S(1)}, f32[256]{0:T(256)S(1)}, u32[]{:S(2)}, u32[]{:S(2)}) collective-permute-start(f32[256]{0:T(256)S(1)} %pad_maximum_fusion), channel_id=1, source_target_pairs={{0,2},{4,6},{1,3},{5,7},{8,10},{12,14},{9,11},{13,15},{16,18},{20,... | collective-permute-start | bytes 3080 | tf_op jit(solution)/shard_map/ppermute | solution.py:28
  60.5 14.9 %collective-permute-start.4 = (f32[256]{0:T(256)S(1)}, f32[256]{0:T(256)S(1)}, u32[]{:S(2)}, u32[]{:S(2)}) collective-permute-start(f32[256]{0:T(256)S(1)} %pad_maximum_fusion.1), channel_id=1, source_target_pairs={{6,4},{7,5},{14,12},{15,13},{22,20},{23,21},{30,28},{31,29},{38,36... | collective-permute-start | bytes 3080 | tf_op jit(solution)/shard_map/ppermute | solution.py:28
  61.2 14.2 %collective-permute-start.5 = (f32[128]{0:T(128)S(1)}, f32[128]{0:T(128)S(1)}, u32[]{:S(2)}, u32[]{:S(2)}) collective-permute-start(f32[128]{0:T(128)S(1)} %get-tuple-element.37), channel_id=1, source_target_pairs={{4,0},{5,1},{12,8},{13,9},{20,16},{21,17},{28,24},{29,25},{36,32},... | collective-permute-start | bytes 1544 | tf_op jit(solution)/shard_map/ppermute | solution.py:28
  75.4 1.1 %copy-start.7 = (f32[64]{0:T(128)}, f32[64]{0:T(128)S(1)}, u32[]{:S(2)}) copy-start(f32[64]{0:T(128)S(1)} %get-tuple-element.24) | copy-start | bytes 772
